TPU v7x, 32 devices: a whole 2x2x4 slice. The times are simulated.
32 devices in a mesh: rep: 2 (over x), dp: 16 (over y, z, core).
Axes of the slice: x: 2, y: 2, z: 4, core: 2. Of those that a mesh axis runs over, the one named last changes fastest.
Arguments:
- x: bfloat16 [32, 2048, 640], P(('rep', 'dp')), parts along dimension 0
- dy: bfloat16 [32, 2048, 640], P(('rep', 'dp')), parts along dimension 0
- w_gate: bfloat16 [2, 640, 2048], replicated
- w_up: bfloat16 [2, 640, 2048], replicated
- w_down: bfloat16 [2, 2048, 640], replicated
- m_w_gate: float32 [2, 640, 2048], replicated
- m_w_up: float32 [2, 640, 2048], replicated
- m_w_down: float32 [2, 2048, 640], replicated
- v_w_gate: float32 [2, 640, 2048], replicated
- v_w_up: float32 [2, 640, 2048], replicated
- v_w_down: float32 [2, 2048, 640], replicated
Outputs:
- output 1: bfloat16 [4, 640, 2048], P('rep'), parts along dimension 0
- output 2: bfloat16 [4, 640, 2048], P('rep'), parts along dimension 0
- output 3: bfloat16 [4, 2048, 640], P('rep'), parts along dimension 0
- output 4: float32 [4, 640, 2048], P('rep'), parts along dimension 0
- output 5: float32 [4, 640, 2048], P('rep'), parts along dimension 0
- output 6: float32 [4, 2048, 640], P('rep'), parts along dimension 0
- output 7: float32 [4, 640, 2048], P('rep'), parts along dimension 0
- output 8: float32 [4, 640, 2048], P('rep'), parts along dimension 0
- output 9: float32 [4, 2048, 640], P('rep'), parts along dimension 0
There are 2 independent parts. A program takes and returns all parts, laid end to end along the dimension named above; an argument that names none is the same for every part.
All inputs are finite; a program needn't handle non-finite values.
Results may differ from a plain program's by a relative error of at most 0.022.
Values are sent between devices in bfloat16 or wider.
A program may use at most 2.25 GiB of HBM per device.

v0:
```python
import jax
import jax.numpy as jnp
from jax import lax
from jax.sharding import PartitionSpec as P

NAMES = ("w_gate", "w_up", "w_down")


def matmul(a, w):
    return jnp.dot(a, w, preferred_element_type=jnp.float32).astype(jnp.bfloat16)


def normed(h):
    wide = h.astype(jnp.float32)
    scale = lax.rsqrt(jnp.mean(wide**2, -1, keepdims=True) + 1e-6)
    return (wide * scale).astype(jnp.bfloat16)


def layer(h, w):
    a = normed(h)
    gate = jnp.dot(a, w["w_gate"], preferred_element_type=jnp.float32)
    up = jnp.dot(a, w["w_up"], preferred_element_type=jnp.float32)
    return h + matmul((jax.nn.silu(gate) * up).astype(jnp.bfloat16), w["w_down"])


def adamw(w, m, v, g):
    m = 0.9 * m + 0.1 * g
    v = 0.95 * v + 0.05 * g * g
    step = m * lax.rsqrt(v + 1e-8) + 0.1 * w
    return (w - 0.02 * step).astype(jnp.bfloat16), m, v


def clipped(gradients, sum_of_squares, count):
    factor = jnp.minimum(1.0, 0.5 * lax.rsqrt(sum_of_squares / count + 1e-30))
    return [g * factor for g in gradients]


def solution(mesh):
    def step(x, dy, *arrays):
        weights, m, v = (arrays[i : i + 3] for i in (0, 3, 6))
        layers = weights[0].shape[0]
        h, kept = x[0], []
        for number in range(layers):
            kept.append(h)
            h = layer(h, {name: w[number] for name, w in zip(NAMES, weights, strict=True)})
        by_h, summed = dy[0], [None] * layers
        for number in reversed(range(layers)):
            _, back = jax.vjp(lambda w, h: layer(h, w), {name: w[number] for name, w in zip(NAMES, weights, strict=True)}, kept[number])
            by_w, by_h = back(by_h)
            summed[number] = [lax.psum(by_w[name], "dp") for name in NAMES]
        gradients = [jnp.stack([summed[number][i] for number in range(layers)]).astype(jnp.float32) for i in range(3)]
        gradients = clipped(gradients, sum(jnp.sum(g * g) for g in gradients), sum(g.size for g in gradients))
        new = [adamw(w.astype(jnp.float32), m, v, g) for w, m, v, g in zip(weights, m, v, gradients, strict=True)]
        return tuple(one[which] for which in range(3) for one in new)

    return jax.shard_map(
        step,
        mesh=mesh,
        in_specs=(P(("rep", "dp"), None, None),) * 2 + (P(None, None, None),) * 9,
        out_specs=(P("rep", None, None),) * 9,
        check_vma=False,
    )
```

profile of v0, /device:TPU:0, one launch (start us, length us, event | category | flops | bytes accessed | tf_op | source)
XLA Modules:
  0.0 583.8 jit_solution(3662924024394976896)
XLA Ops:
  7.2 0.0 all-reduce.3.cloned.1.call-start
  7.2 3.0 copy.20
  10.2 0.0 copy-start.2
  10.2 0.6 fusion.36
  10.8 0.0 copy-start.11
  10.8 4.7 copy.21
  15.5 0.0 copy-start.8
  15.5 11.3 %convolution_convert_fusion.1 = bf16[2048,2048]{1,0:T(8,128)(2,1)} fusion(bf16[1,2048,640]{2,1,0:T(8,128)(2,1)} %param.12, bf16[2,2048,640]{2,1,0:T(8,128)(2,1)} %param.15), kind=kOutput, calls=%fused_computation.65 | convolution fusion | flops 5372903424 | bytes 13631488 | tf_op jit(solution)/shard_map/transpose(jvp())/dot_general | solution.py:10
  26.8 0.0 copy-done.8
  26.8 11.6 %fusion.74 = f32[2048,2048]{1,0:T(8,128)} fusion(bf16[2,640,2048]{2,1,0:T(8,128)(2,1)} %param.13, bf16[1,2048,640]{2,1,0:T(8,128)(2,1)S(1)} %copy-done.8, f32[2048]{0:T(1024)S(1)} %add_rsqrt_fusion), kind=kOutput, calls=%fused_computation.110 | convolution fusion | flops 5372641280 | bytes 22028288 | tf_op jit(solution)/shard_map/dot_general | solution.py:21
  38.4 0.0 copy-done.11
  38.4 16.9 %multiply_convert_fusion.1 = (bf16[2048,2048]{1,0:T(8,128)(2,1)}, f32[2048,2048]{1,0:T(8,128)}) fusion(f32[2048,2048]{1,0:T(8,128)} %fusion.74, bf16[2,640,2048]{2,1,0:T(8,128)(2,1)} %param.14, bf16[1,2048,640]{2,1,0:T(8,128)(2,1)} %param.11, f32[2048]{0:T(1024)S(1)} %add_rsqrt_fusion), kind=kOutput, calls=%fused_computation.17 | convolution fusion | flops 5397807104 | bytes 47194112 | tf_op jit(solution)/shard_map/dot_general | solution.py:22
  55.3 0.0 copy-done.2
  55.3 9.2 %fusion.40 = (f32[2048]{0:T(1024)S(1)}, bf16[2048,640]{0,1:T(8,128)(2,1)S(1)}) fusion(bf16[2048,2048]{1,0:T(8,128)(2,1)} %get-tuple-element.24, bf16[2,2048,640]{2,1,0:T(8,128)(2,1)} %param.15, bf16[1,2048,640]{1,2,0:T(8,128)(2,1)S(1)} %copy.20), kind=kOutput, calls=%fused_computation.73 | convolution fusion | flops 5375260672 | bytes 16261120 | tf_op jit(solution)/shard_map/dot_general | solution.py:10
  64.5 0.0 copy-start.6
  64.5 0.0 copy-start.9
  64.5 1.5 copy-done.6
  66.0 0.0 copy-done.9
  66.0 12.2 %fusion.63 = f32[2048,2048]{1,0:T(8,128)} fusion(bf16[2,640,2048]{2,1,0:T(8,128)(2,1)} %param.14, bf16[2048,640]{0,1:T(8,128)(2,1)S(1)} %get-tuple-element.27, f32[2048]{0:T(1024)S(1)} %fusion.98), kind=kOutput, calls=%fused_computation.99 | convolution fusion | flops 5372641280 | bytes 22028288 | tf_op jit(solution)/shard_map/jvp()/dot_general | solution.py:22
  78.1 0.0 slice-start.2
  78.1 25.1 %fusion.2 = (bf16[2048,2048]{1,0:T(8,128)(2,1)}, f32[2048,2048]{1,0:T(8,128)}) fusion(f32[2048,2048]{1,0:T(8,128)} %fusion.63, bf16[2048,2048]{1,0:T(8,128)(2,1)} %convolution_convert_fusion.1, bf16[2,640,2048]{2,1,0:T(8,128)(2,1)} %param.13, bf16[2048,640]{0,1:T(8,128)(2,1)} %copy-done.6, f32[2048]{0:T(1024)S(1)} %fusion.98), kind=kOutput, calls=%fused_computation.8 | convolution fusion | flops 5422972928 | bytes 55582720 | tf_op jit(solution)/shard_map/jvp()/dot_general | solution.py:21
  103.3 0.0 slice-start.3
  103.3 16.9 %fusion.55 = bf16[1,2048,640]{2,1,0:T(8,128)(2,1)} fusion(f32[2048,2048]{1,0:T(8,128)} %fusion.63, bf16[1,2048,640]{2,1,0:T(8,128)(2,1)} %param.12, f32[2048,2048]{1,0:T(8,128)} %get-tuple-element.29), kind=kOutput, calls=%fused_computation.91 | convolution fusion | flops 5395185664 | bytes 38797312 | tf_op jit(solution)/shard_map/transpose(jvp())/dot_general | solution.py:10
  120.2 0.0 slice-start
  120.2 13.3 %fusion.58 = bf16[1,640,2048]{2,1,0:T(8,128)(2,1)} fusion(bf16[2048,2048]{1,0:T(8,128)(2,1)} %convolution_convert_fusion.1, bf16[2048,640]{0,1:T(8,128)(2,1)} %copy-done.6, f32[2048]{0:T(1024)S(1)} %fusion.98, f32[2048,2048]{1,0:T(8,128)} %get-tuple-element.29), kind=kOutput, calls=%fused_computation.94 | convolution fusion | flops 5399117824 | bytes 30416896 | tf_op jit(solution)/shard_map/transpose(jvp())/dot_general | solution.py:22
  133.5 0.0 slice-done.2
  133.5 0.0 slice-done.3
  133.5 0.0 slice-start.1
  133.5 12.4 %fusion.44 = bf16[2048,640]{0,1:T(8,128)(2,1)} fusion(bf16[2048,2048]{1,0:T(8,128)(2,1)} %convolution_convert_fusion.1, bf16[2,640,2048]{2,1,0:T(8,128)(2,1)S(1)} %bitcast.77, f32[2048,2048]{1,0:T(8,128)} %get-tuple-element.29), kind=kOutput, calls=%fused_computation.81 | convolution fusion | flops 5395185664 | bytes 30408704 | tf_op jit(solution)/shard_map/transpose(jvp())/dot_general | solution.py:22
  145.9 0.0 copy-start.7
  145.9 10.9 %fusion.56 = bf16[1,640,2048]{2,1,0:T(8,128)(2,1)} fusion(bf16[2048,2048]{1,0:T(8,128)(2,1)} %get-tuple-element.28, bf16[2048,640]{0,1:T(8,128)(2,1)} %copy-done.6, f32[2048]{0:T(1024)S(1)} %fusion.98), kind=kOutput, calls=%fused_computation.92 | convolution fusion | flops 5372641280 | bytes 13639680 | tf_op jit(solution)/shard_map/transpose(jvp())/dot_general | solution.py:21
  156.8 0.0 slice-done
  156.8 0.0 slice-done.1
  156.8 0.0 copy-done.7
  156.8 0.0 copy-done.14
  156.9 0.0 copy-start.10
  156.9 0.0 copy-start.1
  156.9 8.5 %fusion.42 = (f32[2048]{0:T(1024)S(1)}, bf16[2048,640]{0,1:T(8,128)(2,1)S(1)}) fusion(bf16[2048,640]{0,1:T(8,128)(2,1)S(1)} %copy-done.7, bf16[2048,640]{0,1:T(8,128)(2,1)S(1)} %copy-done.14, bf16[2048,2048]{1,0:T(8,128)(2,1)} %get-tuple-element.28, bf16[2,640,2048]{2,1,0:T(8,128)(2,1)S(1)} %bitcast.75), kind=kOutput, calls=%fused_computation.75 | convolution fusion | flops 5375260672 | bytes 18882560 | tf_op jit(solution)/shard_map/transpose(jvp())/dot_general | solution.py:21
  165.4 0.0 copy-done.10
  165.4 0.0 copy-done.1
  165.4 0.0 slice-start.4
  165.4 2.0 fusion.60
  167.4 0.0 slice-start.5
  167.5 10.5 %fusion.57 = bf16[1,2048,640]{2,1,0:T(8,128)(2,1)} fusion(bf16[2048,2048]{1,0:T(8,128)(2,1)} %get-tuple-element.24, bf16[2048,640]{0,1:T(8,128)(2,1)S(1)} %fusion.60), kind=kOutput, calls=%fused_computation.93 | convolution fusion | flops 5370019840 | bytes 13631488 | tf_op jit(solution)/shard_map/transpose(jvp())/dot_general | solution.py:10
  177.9 0.0 slice-done.4
  177.9 0.0 slice-done.5
  178.0 0.0 copy-start.12
  178.0 7.3 %convolution_convert_fusion = bf16[2048,2048]{1,0:T(8,128)(2,1)S(1)} fusion(bf16[2048,640]{0,1:T(8,128)(2,1)S(1)} %fusion.60, bf16[2,2048,640]{2,1,0:T(8,128)(2,1)S(1)} %bitcast.79), kind=kOutput, calls=%fused_computation.64 | convolution fusion | flops 5372903424 | bytes 13631488 | tf_op jit(solution)/shard_map/transpose(jvp())/dot_general | solution.py:10
  185.2 0.0 copy-done.3
  185.3 0.0 copy-done.12
  185.3 0.0 copy-start.13
  185.3 13.9 %fusion.51 = bf16[1,640,2048]{2,1,0:T(8,128)(2,1)} fusion(bf16[2048,2048]{1,0:T(8,128)(2,1)S(1)} %convolution_convert_fusion, f32[2048,2048]{1,0:T(8,128)} %fusion.74, bf16[1,2048,640]{1,2,0:T(8,128)(2,1)S(1)} %copy-done.3, f32[2048]{0:T(1024)S(1)} %copy-done.12), kind=kOutput, calls=%fused_computation.89 | convolution fusion | flops 5399117824 | bytes 30416896 | tf_op jit(solution)/shard_map/transpose(jvp())/dot_general | solution.py:22
  199.2 0.0 copy-done.13
  199.2 19.2 %fusion.52 = bf16[1,640,2048]{2,1,0:T(8,128)(2,1)} fusion(f32[2048,2048]{1,0:T(8,128)} %fusion.74, f32[2048,2048]{1,0:T(8,128)} %get-tuple-element.25, bf16[2048,2048]{1,0:T(8,128)(2,1)} %copy-done.13, bf16[1,2048,640]{1,2,0:T(8,128)(2,1)S(1)} %copy-done.3, f32[2048]{0:T(1024)S(1)} %copy-done.12), kind=kOutput, calls=%fused_computation.90 | convolution fusion | flops 5420089344 | bytes 47194112 | tf_op jit(solution)/shard_map/transpose(jvp())/dot_general | solution.py:21
  218.4 0.0 all-reduce.3.cloned.1.call-update
  218.5 283.4 %all-reduce.3.cloned.1.call-done = (bf16[1,640,2048]{2,1,0:T(8,128)(2,1)}, bf16[1,640,2048]{2,1,0:T(8,128)(2,1)}, bf16[1,640,2048]{2,1,0:T(8,128)(2,1)}, bf16[1,...) async-done(((bf16[1,640,2048]{2,1,0:T(8,128)(2,1)}, bf16[1,640,2048]{2,1,0:T(8,128)(2,1)}, bf16[1,640,2048]{2,1,0:T(8,128)(2,1)}, ...) | async-done | bytes 15728656 | tf_op jit(solution)/shard_map/psum | solution.py:50
  501.9 6.0 %fusion.24 = f32[]{:T(128)} fusion(bf16[1,2048,640]{2,1,0:T(8,128)(2,1)} %get-tuple-element.13, bf16[1,2048,640]{2,1,0:T(8,128)(2,1)} %get-tuple-element.14), kind=kLoop, calls=%fused_computation.48 | loop fusion | flops 10485759 | bytes 5242884 | tf_op jit(solution)/shard_map/reduce_sum | solution.py:52
  507.8 5.8 fusion.23
  513.7 0.0 copy-done.4
  513.7 0.0 copy-done.5
  513.7 3.3 fusion.22
  519.0 0.0 copy-done
  519.0 21.4 %fusion.30 = (bf16[2,2048,640]{2,1,0:T(8,128)(2,1)}, f32[2,2048,640]{2,1,0:T(8,128)}, f32[2,2048,640]{2,1,0:T(8,128)}) fusion(bf16[2,2048,640]{2,1,0:T(8,128)(2,1)} %param.15, f32[]{:T(128)S(6)} %min_shard_map.3, bf16[1,2048,640]{2,1,0:T(8,128)(2,1)S(1)} %copy-done, bf16[1,2048,640]{2,1,0:T(8,128)(2,1)} %get-tuple-element.14, f32[2,2048,640]{2,1,0:T(8,128)} %param.21, ...), kind=kLoop, calls=%fused_computation.54 | loop fusion | flops 52428800 | bytes 57671684 | tf_op jit(solution)/shard_map/convert_element_type | solution.py:30
  540.4 36.1 %fusion.21 = (bf16[2,640,2048]{2,1,0:T(8,128)(2,1)}, f32[2,640,2048]{2,1,0:T(8,128)}, f32[2,640,2048]{2,1,0:T(8,128)}, bf16[2,640,2048]{2,1,0:T(8,128)(2,1)}, f3...) fusion(bf16[2,640,2048]{2,1,0:T(8,128)(2,1)} %param.13, f32[]{:T(128)S(6)} %min_shard_map.3, ...), kind=kLoop, calls=%fused_computation.45 | loop fusion | flops 104857600 | bytes 115343360 | tf_op jit(solution)/shard_map/convert_element_type | solution.py:30
  (11 shorter events, 0.0 us)
Async XLA Ops:
  7.2 494.7 %all-reduce.3.cloned.1.call-start = ((), (), s32[]{:S(2)}) async-start(), calls=%async_computation | async-start | bytes 31457280 | tf_op jit(solution)/shard_map/psum | solution.py:50
  10.2 45.1 %copy-start.2 = (bf16[1,2048,640]{1,2,0:T(8,128)(2,1)}, bf16[1,2048,640]{1,2,0:T(8,128)(2,1)S(1)}, u32[]{:S(2)}) copy-start(bf16[1,2048,640]{1,2,0:T(8,128)(2,1)S(1)} %copy.20) | copy-start | bytes 7864324
  10.8 27.6 %copy-start.11 = (f32[2048]{0:T(1024)}, f32[2048]{0:T(1024)S(1)}, u32[]{:S(2)}) copy-start(f32[2048]{0:T(1024)S(1)} %add_rsqrt_fusion) | copy-start | bytes 24580
  15.5 11.3 %copy-start.8 = (bf16[1,2048,640]{2,1,0:T(8,128)(2,1)S(1)}, bf16[1,2048,640]{2,1,0:T(8,128)(2,1)}, u32[]{:S(2)}) copy-start(bf16[1,2048,640]{2,1,0:T(8,128)(2,1)} %param.11) | copy-start | bytes 7864324
  64.5 1.5 copy-start.6
  64.5 1.5 copy-start.9
  78.1 55.4 %slice-start.2 = ((s8[5242880]{0:T(1024)(128)(4,1)}), s8[1048576]{0:T(1024)(128)(4,1)S(1)}, s32[]{:S(2)}) async-start(s8[5242880]{0:T(1024)(128)(4,1)} %bitcast.76), calls=%async_computation.3 | async-start | bytes 2097152
  103.3 30.2 %slice-start.3 = ((s8[5242880]{0:T(1024)(128)(4,1)}), s8[4194304]{0:T(1024)(128)(4,1)S(1)}, s32[]{:S(2)}) async-start(s8[5242880]{0:T(1024)(128)(4,1)} %bitcast.76), calls=%async_computation.4 | async-start | bytes 8388608
  120.2 36.7 %slice-start = ((s8[5242880]{0:T(1024)(128)(4,1)}), s8[4194304]{0:T(1024)(128)(4,1)S(1)}, s32[]{:S(2)}) async-start(s8[5242880]{0:T(1024)(128)(4,1)} %bitcast.74), calls=%async_computation.1 | async-start | bytes 8388608
  133.5 23.3 %slice-start.1 = ((s8[5242880]{0:T(1024)(128)(4,1)}), s8[1048576]{0:T(1024)(128)(4,1)S(1)}, s32[]{:S(2)}) async-start(s8[5242880]{0:T(1024)(128)(4,1)} %bitcast.74), calls=%async_computation.2 | async-start | bytes 2097152
  145.9 10.9 %copy-start.7 = (bf16[2048,640]{0,1:T(8,128)(2,1)S(1)}, bf16[2048,640]{0,1:T(8,128)(2,1)}, u32[]{:S(2)}) copy-start(bf16[2048,640]{0,1:T(8,128)(2,1)} %copy-done.6) | copy-start | bytes 7864324
  145.9 10.9 %copy-start.14 = (bf16[2048,640]{0,1:T(8,128)(2,1)S(1)}, bf16[2048,640]{0,1:T(8,128)(2,1)}, u32[]{:S(2)}) copy-start(bf16[2048,640]{0,1:T(8,128)(2,1)} %fusion.44) | copy-start | bytes 7864324
  156.9 8.5 %copy-start.10 = (f32[2048]{0:T(1024)S(1)}, f32[2048]{0:T(1024)}, u32[]{:S(2)}) copy-start(f32[2048]{0:T(1024)} %copy-done.9) | copy-start | bytes 24580
  156.9 8.5 %copy-start.1 = (bf16[1,2048,640]{1,2,0:T(8,128)(2,1)S(1)}, bf16[1,2048,640]{1,2,0:T(8,128)(2,1)}, u32[]{:S(2)}) copy-start(bf16[1,2048,640]{1,2,0:T(8,128)(2,1)} %copy.21) | copy-start | bytes 7864324
  165.4 12.5 %slice-start.4 = ((s8[5242880]{0:T(1024)(128)(4,1)}), s8[1048576]{0:T(1024)(128)(4,1)S(1)}, s32[]{:S(2)}) async-start(s8[5242880]{0:T(1024)(128)(4,1)} %bitcast.78), calls=%async_computation.5 | async-start | bytes 2097152
  167.4 10.5 %slice-start.5 = ((s8[5242880]{0:T(1024)(128)(4,1)}), s8[4194304]{0:T(1024)(128)(4,1)S(1)}, s32[]{:S(2)}) async-start(s8[5242880]{0:T(1024)(128)(4,1)} %bitcast.78), calls=%async_computation.6 | async-start | bytes 8388608
  177.9 7.3 %copy-start.3 = (bf16[1,2048,640]{1,2,0:T(8,128)(2,1)S(1)}, bf16[1,2048,640]{1,2,0:T(8,128)(2,1)}, u32[]{:S(2)}) copy-start(bf16[1,2048,640]{1,2,0:T(8,128)(2,1)} %copy-done.2) | copy-start | bytes 7864324
  178.0 7.3 %copy-start.12 = (f32[2048]{0:T(1024)S(1)}, f32[2048]{0:T(1024)}, u32[]{:S(2)}) copy-start(f32[2048]{0:T(1024)} %copy-done.11) | copy-start | bytes 24580
  185.3 13.9 %copy-start.13 = (bf16[2048,2048]{1,0:T(8,128)(2,1)}, bf16[2048,2048]{1,0:T(8,128)(2,1)S(1)}, u32[]{:S(2)}) copy-start(bf16[2048,2048]{1,0:T(8,128)(2,1)S(1)} %convolution_convert_fusion) | copy-start | bytes 25165828
  501.9 11.8 %copy-start.4 = (bf16[1,640,2048]{2,1,0:T(8,128)(2,1)S(1)}, bf16[1,640,2048]{2,1,0:T(8,128)(2,1)}, u32[]{:S(2)}) copy-start(bf16[1,640,2048]{2,1,0:T(8,128)(2,1)} %get-tuple-element.9) | copy-start | bytes 7864324
  501.9 11.8 %copy-start.5 = (bf16[1,640,2048]{2,1,0:T(8,128)(2,1)S(1)}, bf16[1,640,2048]{2,1,0:T(8,128)(2,1)}, u32[]{:S(2)}) copy-start(bf16[1,640,2048]{2,1,0:T(8,128)(2,1)} %get-tuple-element.10) | copy-start | bytes 7864324
  501.9 17.1 %copy-start = (bf16[1,2048,640]{2,1,0:T(8,128)(2,1)S(1)}, bf16[1,2048,640]{2,1,0:T(8,128)(2,1)}, u32[]{:S(2)}) copy-start(bf16[1,2048,640]{2,1,0:T(8,128)(2,1)} %get-tuple-element.13) | copy-start | bytes 7864324
Sparse Core Ops, SparseCore 0:
  218.6 283.2 all-reduce.2
where the time goes:
time: 593 us; the launch traced here: 584 us
  waiting for transfers between devices  283 us (48%)
  matrix products  199 us (34%)
  other arithmetic  75.3 us (13%)
  between operations  16.7 us (3%)
  local copies, waits for them, and re-layouts  9.26 us (2%)
    psum x1, waiting for transfers between devices, step(): summed[number] = [lax.psum(by_w[name], 'dp') for name in NAMES]  283 us
    dot_general x5, matrix products, layer(): gate = jnp.dot(a, w['w_gate'], preferred_element_type=jnp.float32)  75.4 us
    dot_general x5, matrix products, layer(): up = jnp.dot(a, w['w_up'], preferred_element_type=jnp.float32)  68.7 us
    convert_element_type x2, other arithmetic, adamw(): return ((w - 0.02 * step).astype(jnp.bfloat16), m, v)  57.6 us
    dot_general x5, matrix products, matmul(): jnp.dot(a, w, preferred_element_type=jnp.float32).astype(jnp.bfloat16)  55.1 us
    reduce_sum x3, other arithmetic, step(): jnp.sum(g * g)  15.1 us
  transfers between devices with their start and end apart: 1, of which 1 were waited for; matrix products, arithmetic and copies ran while one was open for 0% of the time, Pallas kernels for 0%

commit v1 on v0

v1 whole, which is shorter than its diff:
```python
import jax
import jax.numpy as jnp
from jax import lax
from jax.experimental import pallas as pl
from jax.experimental.pallas import tpu as pltpu
from jax.sharding import PartitionSpec as P

T, D, FF, LAYERS = 2048, 640, 2048, 2
RING = 8
TILE = FF // RING
HALF = D // 2
ROWS = 512
BF, F32 = jnp.bfloat16, jnp.float32
MESH = pl.DeviceIdType.MESH


def dot(a, b, ca, cb):
    return lax.dot_general(a, b, (((ca,), (cb,)), ((), ())), preferred_element_type=F32)


def step_kernel(
    x_hbm, dy_hbm, wg_hbm, wu_hbm, wd_hbm, g_out, ss_out,
    H, A, AT, DY, DYT, ACC, HID, DG, DU, WG, WU, WD, G, R, L, PS,
    wsem, xsem, osem, p_s, p_r, rs_s, rs_r, ag_s, ag_r, ap_s, ap_r, free,
):
    me = lax.axis_index("dp")
    core = me % 2
    y, z = me // 8, (me // 2) % 4
    pos = z + y * (7 - 2 * z)

    def device(position, c):
        yy = position // 4
        zz = position - yy * (2 * position - 7)
        return {"dp": yy * 8 + zz * 2 + c}

    partner = device(pos, 1 - core)

    def chunk(k):
        return (pos + 8 + (4 - (k + 1) // 2) * (2 * (k % 2) - 1)) % RING

    def weight_copies(layer, k):
        at = pl.ds(pl.multiple_of(chunk(k) * TILE, TILE), TILE)
        slot = k % 2
        return (
            pltpu.make_async_copy(wg_hbm.at[layer, :, at], WG.at[slot], wsem.at[slot, 0]),
            pltpu.make_async_copy(wu_hbm.at[layer, :, at], WU.at[slot], wsem.at[slot, 1]),
            pltpu.make_async_copy(wd_hbm.at[layer, at, :], WD.at[slot], wsem.at[slot, 2]),
        )

    def start_weights(layer, k):
        for c in weight_copies(layer, k):
            c.start()

    def next_weights(layer, k):
        for c in weight_copies(layer, k):
            c.wait()

        @pl.when(k < RING - 1)
        def _():
            start_weights(layer, k + 1)

    x_copy = pltpu.make_async_copy(x_hbm, H, xsem.at[0])
    dy_copy = pltpu.make_async_copy(dy_hbm, DY, xsem.at[1])
    x_copy.start()
    dy_copy.start()
    start_weights(0, 0)

    barrier = pltpu.get_barrier_semaphore()
    for other in (partner, device((pos + 1) % RING, core), device((pos + 7) % RING, core)):
        pl.semaphore_signal(barrier, inc=1, device_id=other, device_id_type=MESH)
    pl.semaphore_wait(barrier, 3)

    def rows(r, n=ROWS):
        return pl.ds(pl.multiple_of(r * n, n), n)

    def normed_into(dst):
        @pl.loop(0, T // 128)
        def _(r):
            at = rows(r, 128)
            wide = H[at, :].astype(F32)
            scale = lax.rsqrt(jnp.mean(wide * wide, -1, keepdims=True) + 1e-6)
            dst[at, :] = (wide * scale).astype(BF)

    def transposed_into(dst, src):
        @pl.loop(0, T // 128)
        def _(r):
            at = rows(r, 128)
            dst[:, at] = src[at, :].T

    def partner_copy(layer, k):
        p = chunk(k)
        return pltpu.make_async_remote_copy(
            src_ref=G.at[layer, p, 1 - core], dst_ref=R.at[layer, p],
            send_sem=p_s.at[layer, k], recv_sem=p_r.at[layer, k], device_id=partner, device_id_type=MESH,
        )

    def ring_copy(layer, k, sign):
        return pltpu.make_async_remote_copy(
            src_ref=R.at[layer, chunk(k)], dst_ref=L.at[layer, k],
            send_sem=rs_s.at[layer, k], recv_sem=rs_r.at[layer, k],
            device_id=device((pos + RING + sign) % RING, core), device_id_type=MESH,
        )

    def add_up(layer, k, came, dst):
        p = chunk(k)
        for m in range(3):

            @pl.loop(0, HALF // 64)
            def _(r):
                at = rows(r, 64)
                total = G[layer, p, core, m, at, :].astype(F32) + R[layer, p, m, at, :].astype(F32)
                for j in came:
                    total += L[layer, j, m, at, :].astype(F32)
                dst[layer, p, m, at, :] = total.astype(BF)

    def reduce_step(layer, k):
        partner_copy(layer, k).wait()
        first = (k == 0) | ((k == 1) & (core == 1)) | ((k == 2) & (core == 0))
        late = k >= 3

        @pl.when(first)
        def _():
            add_up(layer, k, (), R)

        @pl.when((k == 1) & (core == 0) | (k == 2) & (core == 1))
        def _():
            ring_copy(layer, 0, 1).wait_recv()
            add_up(layer, k, (0,), R)

        @pl.when(late)
        def _():
            ring_copy(layer, k - 2, 1).wait_recv()
            add_up(layer, k, (k - 2,), R)

        @pl.when(k == 0)
        def _():
            ring_copy(layer, k, 1 - 2 * core).start()

        @pl.when(k > 0)
        def _():
            ring_copy(layer, k, 2 * (k % 2) - 1).start()

    def reduce_last(layer):
        partner_copy(layer, 7).wait()
        pl.semaphore_signal(free.at[layer], inc=1, device_id=partner, device_id_type=MESH)
        ring_copy(layer, 5, 1).wait_recv()
        ring_copy(layer, 6, 1).wait_recv()
        for m in range(3):

            @pl.loop(0, HALF // 64)
            def _(r):
                at = rows(r, 64)
                total = G[layer, pos, core, m, at, :].astype(F32) + R[layer, pos, m, at, :].astype(F32)
                total += L[layer, 5, m, at, :].astype(F32)
                total += L[layer, 6, m, at, :].astype(F32)
                G[layer, pos, core, m, at, :] = total.astype(BF)

        pl.semaphore_wait(free.at[layer], 1)

    def event_chunk(e):
        return (pos + 8 + ((e + 1) // 2) * (1 - 2 * (e % 2))) % RING

    def gather_copy(layer, e, m, p, sign):
        return pltpu.make_async_remote_copy(
            src_ref=G.at[layer, p, core, m], dst_ref=G.at[layer, p, core, m],
            send_sem=ag_s.at[layer, e, m], recv_sem=ag_r.at[layer, e, m],
            device_id=device((pos + RING + sign) % RING, core), device_id_type=MESH,
        )

    def share_copy(layer, e, c):
        p = event_chunk(e)
        return pltpu.make_async_remote_copy(
            src_ref=G.at[layer, p, c], dst_ref=G.at[layer, p, c],
            send_sem=ap_s.at[layer, e], recv_sem=ap_r.at[layer, e], device_id=partner, device_id_type=MESH,
        )

    def gather_event(layer, e):
        p = event_chunk(e)

        @pl.when(e == 0)
        def _():
            for m in range(3):
                gather_copy(layer, 1, m, p, 1).start()
                gather_copy(layer, 2, m, p, -1).start()

        @pl.when(e > 0)
        def _():
            for m in range(3):
                gather_copy(layer, e, m, p, 1).wait_recv()

                @pl.when((e <= 4) | ((e == 5) & (core == 0)))
                def _():
                    gather_copy(layer, e + 2, m, p, 2 * (e % 2) - 1).start()

                @pl.when((e == 6) & (core == 1))
                def _():
                    gather_copy(layer, 7, m, p, -1).start()

        share_copy(layer, e, core).start()

    def out_copy(layer, e):
        p = event_chunk(e)
        return pltpu.make_async_copy(G.at[layer, p], g_out.at[layer, p], osem.at[layer, e])

    def squares(layer, e):
        share_copy(layer, e, 1 - core).wait_recv()
        out_copy(layer, e).start()
        p = event_chunk(e)
        total = jnp.zeros((8, TILE), F32)
        for c in range(2):
            for m in range(3):

                def add(r, total):
                    wide = G[layer, p, c, m, rows(r, 64), :].astype(F32)
                    return total + jnp.sum((wide * wide).reshape(8, 8, TILE), 0)

                total = lax.fori_loop(0, HALF // 64, add, total)
        PS[layer, p] = total

    x_copy.wait()
    normed_into(A)

    @pl.loop(0, RING)
    def _(k):
        next_weights(0, k)
        slot = k % 2

        @pl.loop(0, T // ROWS)
        def _(r):
            at = rows(r)
            gate = dot(A[at, :], WG[slot], 1, 0)
            up = dot(A[at, :], WU[slot], 1, 0)
            hid = (gate * jax.nn.sigmoid(gate) * up).astype(BF)
            part = dot(hid, WD[slot], 1, 0)

            @pl.when(k == 0)
            def _():
                ACC[at, :] = part

            @pl.when(k > 0)
            def _():
                ACC[at, :] += part

    start_weights(1, 0)

    @pl.loop(0, T // 128)
    def _(r):
        at = rows(r, 128)
        H[at, :] = (H[at, :].astype(F32) + ACC[at, :].astype(BF).astype(F32)).astype(BF)

    normed_into(A)
    transposed_into(AT, A)
    dy_copy.wait()
    transposed_into(DYT, DY)

    def tile(layer, k):
        next_weights(layer, k)
        slot = k % 2

        @pl.loop(0, T // ROWS)
        def _(r):
            at = rows(r)
            gate = dot(A[at, :], WG[slot], 1, 0)
            up = dot(A[at, :], WU[slot], 1, 0)
            by_hid = dot(DY[at, :], WD[slot], 1, 1).astype(BF).astype(F32)
            sig = jax.nn.sigmoid(gate)
            silu = gate * sig
            HID[at, :] = (silu * up).astype(BF)
            by_up = (by_hid * silu).astype(BF)
            by_gate = (by_hid * up * (sig + silu * (1.0 - sig))).astype(BF)
            DU[at, :] = by_up
            DG[at, :] = by_gate
            if layer == 1:
                part = dot(by_gate, WG[slot], 1, 1) + dot(by_up, WU[slot], 1, 1)

                @pl.when(k == 0)
                def _():
                    ACC[at, :] = part

                @pl.when(k > 0)
                def _():
                    ACC[at, :] += part

        p = chunk(k)
        for m, left, right in ((0, AT, DG), (1, AT, DU), (2, DYT, HID)):

            @pl.loop(0, 2)
            def _(half):
                g = dot(left[rows(half, HALF), :], right[...], 1, 0)
                G[layer, p, half, m] = g.astype(BF)

        partner_copy(layer, k).start()

    @pl.loop(0, RING)
    def _(k):
        tile(1, k)

        @pl.when(k > 0)
        def _():
            reduce_step(1, k - 1)

    start_weights(0, 0)

    @pl.loop(0, T // 128)
    def _(r):
        at = rows(r, 128)
        by_a = ACC[at, :].astype(BF).astype(F32)
        wide = H[at, :].astype(F32)
        scale = lax.rsqrt(jnp.mean(wide * wide, -1, keepdims=True) + 1e-6)
        along = jnp.mean(by_a * wide, -1, keepdims=True) * (scale * scale)
        by_h = (scale * (by_a - wide * along)).astype(BF).astype(F32)
        DY[at, :] = (DY[at, :].astype(F32) + by_h).astype(BF)

    again = pltpu.make_async_copy(x_hbm, H, xsem.at[0])
    again.start()
    transposed_into(DYT, DY)
    again.wait()
    normed_into(A)
    transposed_into(AT, A)
    reduce_last(1)


    @pl.loop(0, RING)
    def _(k):
        tile(0, k)

        @pl.when(k > 0)
        def _():
            reduce_step(0, k - 1)

        gather_event(1, k)

    reduce_last(0)

    @pl.loop(0, RING)
    def _(e):
        gather_event(0, e)
        squares(1, e)

    @pl.loop(0, RING)
    def _(e):
        squares(0, e)

    total = jnp.zeros((8, TILE), F32)
    for layer in range(LAYERS):
        for p in range(RING):
            total += PS[layer, p]
    ss_out[...] = total

    for layer in range(LAYERS):

        @pl.loop(0, RING)
        def _(k):
            share_copy(layer, k, core).wait_send()
            out_copy(layer, k).wait()

        @pl.loop(0, RING - 1)
        def _(k):
            ring_copy(layer, k, 1).wait_send()
            for m in range(3):
                gather_copy(layer, k + 1, m, event_chunk(k + 1), 1).wait_send()


def update_kernel(ss, g, *refs):
    ins, outs = refs[:9], refs[9:]
    count = float(3 * LAYERS * D * FF)
    factor = jnp.minimum(1.0, 0.5 * lax.rsqrt(jnp.sum(ss[...]) / count + 1e-30))
    for i in range(3):
        w, m, v = ins[3 * i : 3 * i + 3]
        new_w, new_m, new_v = outs[3 * i : 3 * i + 3]
        grad = g[0, 0, :, i].reshape(D, TILE).astype(F32) * factor
        if i == 2:
            grad = grad.T
        mm = 0.9 * m[0] + 0.1 * grad
        vv = 0.95 * v[0] + 0.05 * grad * grad
        wide = w[0].astype(F32)
        new_m[0] = mm
        new_v[0] = vv
        new_w[0] = (wide - 0.02 * (mm * lax.rsqrt(vv + 1e-8) + 0.1 * wide)).astype(BF)


def solution(mesh):
    any_ = pl.BlockSpec(memory_space=pl.ANY)
    chunk_of = (3, HALF, TILE)
    dma = pltpu.SemaphoreType.DMA

    gradients = pl.pallas_call(
        step_kernel,
        name="gradients",
        out_shape=(
            jax.ShapeDtypeStruct((LAYERS, RING, 2, *chunk_of), BF),
            jax.ShapeDtypeStruct((8, TILE), F32),
        ),
        in_specs=[any_] * 5,
        out_specs=(any_, pl.BlockSpec(memory_space=pltpu.VMEM)),
        scratch_shapes=[
            pltpu.VMEM((T, D), BF), pltpu.VMEM((T, D), BF), pltpu.VMEM((D, T), BF), pltpu.VMEM((T, D), BF), pltpu.VMEM((D, T), BF),
            pltpu.VMEM((T, D), F32),
            pltpu.VMEM((T, TILE), BF), pltpu.VMEM((T, TILE), BF), pltpu.VMEM((T, TILE), BF),
            pltpu.VMEM((2, D, TILE), BF), pltpu.VMEM((2, D, TILE), BF), pltpu.VMEM((2, TILE, D), BF),
            pltpu.VMEM((LAYERS, RING, 2, *chunk_of), BF),
            pltpu.VMEM((LAYERS, RING, *chunk_of), BF),
            pltpu.VMEM((LAYERS, RING - 1, *chunk_of), BF),
            pltpu.VMEM((LAYERS, RING, 8, TILE), F32),
            dma((2, 3)), dma((2,)), dma((LAYERS, RING)),
            dma((LAYERS, RING)), dma((LAYERS, RING)),
            dma((LAYERS, RING - 1)), dma((LAYERS, RING - 1)),
            dma((LAYERS, RING, 3)), dma((LAYERS, RING, 3)),
            dma((LAYERS, RING)), dma((LAYERS, RING)), pltpu.SemaphoreType.REGULAR((LAYERS,)),
        ],
        compiler_params=pltpu.CompilerParams(collective_id=0, has_side_effects=True, vmem_limit_bytes=67_043_328),
    )

    wide = pl.BlockSpec((1, D, TILE), lambda l, p: (l, 0, p))
    tall = pl.BlockSpec((1, TILE, D), lambda l, p: (l, p, 0))
    specs = [wide] * 6 + [tall] * 3
    up_shape, down_shape = (LAYERS, D, FF), (LAYERS, FF, D)
    shapes = [jax.ShapeDtypeStruct(s, t) for s in (up_shape, up_shape, down_shape) for t in (BF, F32, F32)]
    update = pl.pallas_call(
        update_kernel,
        name="update",
        grid=(LAYERS, RING),
        out_shape=shapes,
        in_specs=[pl.BlockSpec((8, TILE), lambda l, p: (0, 0)), pl.BlockSpec((1, 1, 2, *chunk_of), lambda l, p: (l, p, 0, 0, 0, 0))] + specs,
        out_specs=specs,
        compiler_params=pltpu.CompilerParams(vmem_limit_bytes=60_000_000),
    )

    def step(x, dy, wg, wu, wd, mg, mu, md, vg, vu, vd):
        g, ss = gradients(x[0], dy[0], wg, wu, wd)
        new = update(ss, g, wg, mg, vg, wu, mu, vu, wd, md, vd)
        return tuple(new[3 * i + which] for which in range(3) for i in range(3))

    return jax.shard_map(
        step,
        mesh=mesh,
        in_specs=(P(("rep", "dp"), None, None),) * 2 + (P(None, None, None),) * 9,
        out_specs=(P("rep", None, None),) * 9,
        check_vma=False,
    )
```

time: 593 us -> 339 us (0.57); the launches traced: 584 us -> 339 us
  Pallas kernels: 0 us -> 338 us
  waiting for transfers between devices: 283 us -> 0 us
  matrix products: 199 us -> 0 us
  other arithmetic: 75.3 us -> 0 us
  between operations: 16.7 us -> 0.65 us
  local copies, waits for them, and re-layouts: 9.26 us -> 0 us
    pallas_call x0 -> x2, Pallas kernels: none -> 338 us  [the longest x1 281 us: step(): g, ss = gradients(x[0], dy[0], wg, wu, wd)]
    psum x1 -> x0, waiting for transfers between devices: 283 us -> none  [step(): summed[number] = [lax.psum(by_w[name], 'dp') for name in NAMES]]
    dot_general x15 -> x0, matrix products: 199 us -> none  [the longest x5 75.4 us: layer(): gate = jnp.dot(a, w['w_gate'], preferred_element_type=jnp.float32)]
    convert_element_type x2 -> x0, other arithmetic: 57.6 us -> none  [adamw(): return ((w - 0.02 * step).astype(jnp.bfloat16), m, v)]
    reduce_sum x4 -> x0, other arithmetic: 15.7 us -> none  [the longest x3 15.1 us: step(): jnp.sum(g * g)]
    unnamed x44 -> x0, local copies, waits for them, and re-layouts: 9.26 us -> none
  transfers between devices with their start and end apart: 1 -> 0, of which waited for: 1 -> 0; matrix products, arithmetic and copies ran while one was open for 0% -> 0% of each run, Pallas kernels for 0% -> 0%
where the time goes in v1:
time: 339 us
  Pallas kernels  338 us (100%)
    pallas_call x1, Pallas kernels, step(): g, ss = gradients(x[0], dy[0], wg, wu, wd)  281 us
    pallas_call x1, Pallas kernels, step(): new = update(ss, g, wg, mg, vg, wu, mu, vu, wd, md, vd)  57 us

profile of v1, /device:TPU:0, one launch (start us, length us, event | category | flops | bytes accessed | tf_op | source)
XLA Modules:
  0.0 338.8 jit_solution(285728322207846324)
XLA Ops:
  0.6 281.2 %gradients.1 = (bf16[2,8,2,3,320,256]{5,4,3,2,1,0:T(8,128)(2,1)}, f32[8,256]{1,0:T(8,128)}) custom-call(bf16[2048,640]{1,0:T(8,128)(2,1)} %bitcast.2, bf16[2048,640]{1,0:T(8,128)(2,1)} %bitcast.3, bf16[2,640,2048]{2,1,0:T(8,128)(2,1)} %refs_0_.1, bf16[2,640,2048]{2,1,0:T(8,128)(2,1)} %refs_3_.1, bf16[2,2048,640]{2,1,0:T(8,128)(2,1)} %refs_6_.1), custom_call_target="tpu_custom_call" | custom-call | tf_op jit(solution)/shard_map/gradients/pallas_call | solution.py:430
  281.8 57.0 %update.1 = (bf16[2,640,2048]{2,1,0:T(8,128)(2,1)}, f32[2,640,2048]{2,1,0:T(8,128)}, f32[2,640,2048]{2,1,0:T(8,128)}, bf16[2,640,2048]{2,1,0:T(8,128)(2,1)}, f32...) custom-call(f32[8,256]{1,0:T(8,128)} %get-tuple-element.20.ss, ...), custom_call_target="tpu_custom_call" | custom-call | tf_op jit(solution)/shard_map/update/pallas_call | solution.py:431

commit v2 on v1

v2 whole, which is shorter than its diff:
```python
import jax
import jax.numpy as jnp
from jax import lax
from jax.experimental import pallas as pl
from jax.experimental.pallas import tpu as pltpu
from jax.sharding import PartitionSpec as P

T, D, FF, LAYERS = 2048, 640, 2048, 2
RING = 8
TILE = FF // RING
HALF = D // 2
SUB = TILE // 2
PARTS = 2 * LAYERS
ROWS, FEW = 1024, 512
BF, F32 = jnp.bfloat16, jnp.float32
MESH = pl.DeviceIdType.MESH


def dot(a, b, ca, cb):
    return lax.dot_general(a, b, (((ca,), (cb,)), ((), ())), preferred_element_type=F32)


def step_kernel(
    x_hbm, dy_hbm, wg_hbm, wu_hbm, wd_hbm, g_out, ss_out,
    H, A, AT, DY, DYT, ACC, HID, DGU, WGU, WD, G, R, L, PS,
    wsem, xsem, osem, p_s, p_r, rs_s, rs_r, ag_s, ag_r, ap_s, ap_r, free,
):
    me = lax.axis_index("dp")
    core = me % 2
    y, z = me // 8, (me // 2) % 4
    pos = z + y * (7 - 2 * z)

    def device(position, c):
        yy = position // 4
        zz = position - yy * (2 * position - 7)
        return {"dp": yy * 8 + zz * 2 + c}

    partner = device(pos, 1 - core)

    def chunk(k):
        return (pos + 8 + (4 - (k + 1) // 2) * (2 * (k % 2) - 1)) % RING

    def weight_copies(layer, n):
        slot, half = n % 2, n // 4
        copies = []
        for j in range(2):
            at = pl.ds(pl.multiple_of(chunk((2 * n + j) % RING) * TILE + half * SUB, SUB), SUB)
            here = pl.ds(j * SUB, SUB)
            copies += [
                pltpu.make_async_copy(wg_hbm.at[layer, :, at], WGU.at[slot, :, here], wsem.at[slot, 3 * j]),
                pltpu.make_async_copy(wu_hbm.at[layer, :, at], WGU.at[slot, :, pl.ds(TILE + j * SUB, SUB)], wsem.at[slot, 3 * j + 1]),
                pltpu.make_async_copy(wd_hbm.at[layer, at, :], WD.at[slot, here, :], wsem.at[slot, 3 * j + 2]),
            ]
        return copies

    def start_weights(layer, k):
        for c in weight_copies(layer, k):
            c.start()

    def next_weights(layer, k):
        for c in weight_copies(layer, k):
            c.wait()

        @pl.when(k < RING - 1)
        def _():
            start_weights(layer, k + 1)

    x_copy = pltpu.make_async_copy(x_hbm, H, xsem.at[0])
    dy_copy = pltpu.make_async_copy(dy_hbm, DY, xsem.at[1])
    x_copy.start()
    dy_copy.start()
    start_weights(0, 0)

    barrier = pltpu.get_barrier_semaphore()
    for other in (partner, device((pos + 1) % RING, core), device((pos + 7) % RING, core)):
        pl.semaphore_signal(barrier, inc=1, device_id=other, device_id_type=MESH)

    def rows(r, n=ROWS):
        return pl.ds(pl.multiple_of(r * n, n), n)

    def normed_into(dst):
        @pl.loop(0, T // FEW)
        def _(r):
            at = rows(r, FEW)
            wide = H[at, :].astype(F32)
            scale = lax.rsqrt(jnp.mean(wide * wide, -1, keepdims=True) + 1e-6)
            dst[at, :] = (wide * scale).astype(BF)

    def transposed_into(dst, src):
        @pl.loop(0, T // FEW)
        def _(r):
            at = rows(r, FEW)
            dst[:, at] = src[at, :].T

    def partner_copy(part, k):
        p = chunk(k)
        return pltpu.make_async_remote_copy(
            src_ref=G.at[part, p, 1 - core], dst_ref=R.at[part, p],
            send_sem=p_s.at[part, k], recv_sem=p_r.at[part, k], device_id=partner, device_id_type=MESH,
        )

    def ring_copy(part, k, sign):
        return pltpu.make_async_remote_copy(
            src_ref=R.at[part, chunk(k)], dst_ref=L.at[part, k],
            send_sem=rs_s.at[part, k], recv_sem=rs_r.at[part, k],
            device_id=device((pos + RING + sign) % RING, core), device_id_type=MESH,
        )

    def add_up(part, k, came, dst):
        p = chunk(k)
        for m in range(3):

            @pl.loop(0, HALF // 64)
            def _(r):
                at = rows(r, 64)
                total = G[part, p, core, m, at, :].astype(F32) + R[part, p, m, at, :].astype(F32)
                for j in came:
                    total += L[part, j, m, at, :].astype(F32)
                dst[part, p, m, at, :] = total.astype(BF)

    def reduce_step(part, k):
        partner_copy(part, k).wait()
        first = (k == 0) | ((k == 1) & (core == 1)) | ((k == 2) & (core == 0))
        late = k >= 3

        @pl.when(first)
        def _():
            add_up(part, k, (), R)

        @pl.when((k == 1) & (core == 0) | (k == 2) & (core == 1))
        def _():
            ring_copy(part, 0, 1).wait_recv()
            add_up(part, k, (0,), R)

        @pl.when(late)
        def _():
            ring_copy(part, k - 2, 1).wait_recv()
            add_up(part, k, (k - 2,), R)

        @pl.when(k == 0)
        def _():
            ring_copy(part, k, 1 - 2 * core).start()

        @pl.when(k > 0)
        def _():
            ring_copy(part, k, 2 * (k % 2) - 1).start()

    def reduce_last(part):
        partner_copy(part, 7).wait()
        pl.semaphore_signal(free.at[part], inc=1, device_id=partner, device_id_type=MESH)
        ring_copy(part, 5, 1).wait_recv()
        ring_copy(part, 6, 1).wait_recv()
        for m in range(3):

            @pl.loop(0, HALF // 64)
            def _(r):
                at = rows(r, 64)
                total = G[part, pos, core, m, at, :].astype(F32) + R[part, pos, m, at, :].astype(F32)
                total += L[part, 5, m, at, :].astype(F32)
                total += L[part, 6, m, at, :].astype(F32)
                G[part, pos, core, m, at, :] = total.astype(BF)

        pl.semaphore_wait(free.at[part], 1)

    def event_chunk(e):
        return (pos + 8 + ((e + 1) // 2) * (1 - 2 * (e % 2))) % RING

    def gather_copy(part, e, m, p, sign):
        return pltpu.make_async_remote_copy(
            src_ref=G.at[part, p, core, m], dst_ref=G.at[part, p, core, m],
            send_sem=ag_s.at[part, e, m], recv_sem=ag_r.at[part, e, m],
            device_id=device((pos + RING + sign) % RING, core), device_id_type=MESH,
        )

    def share_copy(part, e, c):
        p = event_chunk(e)
        return pltpu.make_async_remote_copy(
            src_ref=G.at[part, p, c], dst_ref=G.at[part, p, c],
            send_sem=ap_s.at[part, e], recv_sem=ap_r.at[part, e], device_id=partner, device_id_type=MESH,
        )

    def gather_event(part, e):
        p = event_chunk(e)

        @pl.when(e == 0)
        def _():
            for m in range(3):
                gather_copy(part, 1, m, p, 1).start()
                gather_copy(part, 2, m, p, -1).start()

        @pl.when(e > 0)
        def _():
            for m in range(3):
                gather_copy(part, e, m, p, 1).wait_recv()

                @pl.when((e <= 4) | ((e == 5) & (core == 0)))
                def _():
                    gather_copy(part, e + 2, m, p, 2 * (e % 2) - 1).start()

                @pl.when((e == 6) & (core == 1))
                def _():
                    gather_copy(part, 7, m, p, -1).start()

        share_copy(part, e, core).start()

    def out_copy(part, e):
        p = event_chunk(e)
        return pltpu.make_async_copy(G.at[part, p], g_out.at[part, p], osem.at[part, e])

    def squares(part, e):
        share_copy(part, e, 1 - core).wait_recv()
        out_copy(part, e).start()
        p = event_chunk(e)
        total = jnp.zeros((8, SUB), F32)
        for c in range(2):
            for m in range(3):

                def add(r, total):
                    wide = G[part, p, c, m, rows(r, 64), :].astype(F32)
                    return total + jnp.sum((wide * wide).reshape(8, 8, SUB), 0)

                total = lax.fori_loop(0, HALF // 64, add, total)
        PS[part, p] = total

    x_copy.wait()
    normed_into(A)

    @pl.loop(0, RING)
    def _(k):
        next_weights(0, k)
        slot = k % 2

        @pl.loop(0, T // ROWS)
        def _(r):
            at = rows(r)
            both = dot(A[at, :], WGU[slot], 1, 0)
            gate, up = both[:, :TILE], both[:, TILE:]
            hid = (gate * jax.nn.sigmoid(gate) * up).astype(BF)
            part = dot(hid, WD[slot], 1, 0)

            @pl.when(k == 0)
            def _():
                ACC[at, :] = part

            @pl.when(k > 0)
            def _():
                ACC[at, :] += part

    start_weights(1, 0)

    @pl.loop(0, T // FEW)
    def _(r):
        at = rows(r, FEW)
        H[at, :] = (H[at, :].astype(F32) + ACC[at, :].astype(BF).astype(F32)).astype(BF)

    normed_into(A)
    transposed_into(AT, A)
    dy_copy.wait()
    transposed_into(DYT, DY)

    def tile(part, n):
        layer = 1 - part // 2
        next_weights(layer, n)
        slot = n % 2

        @pl.loop(0, T // ROWS)
        def _(r):
            at = rows(r)
            both = dot(A[at, :], WGU[slot], 1, 0)
            gate, up = both[:, :TILE], both[:, TILE:]
            by_hid = dot(DY[at, :], WD[slot], 1, 1).astype(BF).astype(F32)
            sig = jax.nn.sigmoid(gate)
            silu = gate * sig
            HID[at, :] = (silu * up).astype(BF)
            DGU[at, pl.ds(TILE, TILE)] = (by_hid * silu).astype(BF)
            DGU[at, pl.ds(0, TILE)] = (by_hid * up * (sig + silu * (1.0 - sig))).astype(BF)

        if layer == 1:

            @pl.loop(0, T // ROWS)
            def _(r):
                at = rows(r)
                term = dot(DGU[at, :], WGU[slot], 1, 1)

                @pl.when(n == 0)
                def _():
                    ACC[at, :] = term

                @pl.when(n > 0)
                def _():
                    ACC[at, :] += term

        settle(part, n % 4)

        for left, right, ms in ((AT, DGU, (0, 1)), (DYT, HID, (2,))):
            g = dot(left[...], right[...], 1, 0).astype(BF)
            for i, m in enumerate(ms):
                for j in range(2):
                    at = slice(i * TILE + j * SUB, i * TILE + (j + 1) * SUB)
                    for half in range(2):
                        G[part, chunk((2 * n + j) % RING), half, m] = g[half * HALF : (half + 1) * HALF, at]

        for j in range(2):
            partner_copy(part, (2 * n + j) % RING).start()

    def settle(part, n):
        @pl.when(n == 0)
        def _():
            if part > 0:
                reduce_step(part - 1, 5)
                reduce_step(part - 1, 6)
            if part > 1:
                gather_event(part - 2, 5)
                gather_event(part - 2, 6)

        @pl.when(n == 1)
        def _():
            reduce_step(part, 0)
            if part > 0:
                reduce_last(part - 1)
                gather_event(part - 1, 0)
            if part > 1:
                gather_event(part - 2, 7)

        @pl.when(n > 1)
        def _():
            reduce_step(part, 2 * n - 3)
            reduce_step(part, 2 * n - 2)
            if part > 0:
                gather_event(part - 1, 2 * n - 3)
                gather_event(part - 1, 2 * n - 2)

    pl.semaphore_wait(barrier, 3)

    for part in range(2):

        @pl.loop(0, 4)
        def _(n):
            tile(part, 4 * part + n)

    start_weights(0, 0)

    @pl.loop(0, T // FEW)
    def _(r):
        at = rows(r, FEW)
        by_a = ACC[at, :].astype(BF).astype(F32)
        wide = H[at, :].astype(F32)
        scale = lax.rsqrt(jnp.mean(wide * wide, -1, keepdims=True) + 1e-6)
        along = jnp.mean(by_a * wide, -1, keepdims=True) * (scale * scale)
        by_h = (scale * (by_a - wide * along)).astype(BF).astype(F32)
        DY[at, :] = (DY[at, :].astype(F32) + by_h).astype(BF)

    again = pltpu.make_async_copy(x_hbm, H, xsem.at[0])
    again.start()
    transposed_into(DYT, DY)
    again.wait()
    normed_into(A)
    transposed_into(AT, A)

    for part in range(2, 4):

        @pl.loop(0, 4)
        def _(n):
            tile(part, 4 * (part - 2) + n)

    reduce_step(3, 5)
    reduce_step(3, 6)
    gather_event(2, 5)
    gather_event(2, 6)

    @pl.loop(0, RING)
    def _(e):
        for part in range(2):
            squares(part, e)

    reduce_last(3)
    gather_event(3, 0)
    gather_event(2, 7)

    @pl.loop(1, RING)
    def _(e):
        squares(2, e - 1)
        gather_event(3, e)
        squares(3, e - 1)

    squares(2, 7)
    squares(3, 7)

    total = jnp.zeros((8, SUB), F32)
    for part in range(PARTS):
        for p in range(RING):
            total += PS[part, p]
    ss_out[...] = total

    for part in range(PARTS):

        @pl.loop(0, RING)
        def _(k):
            share_copy(part, k, core).wait_send()
            out_copy(part, k).wait()

        @pl.loop(0, RING - 1)
        def _(k):
            ring_copy(part, k, 1).wait_send()
            for m in range(3):
                gather_copy(part, k + 1, m, event_chunk(k + 1), 1).wait_send()


def update_kernel(ss, g, *refs):
    ins, outs = refs[:9], refs[9:]
    count = float(3 * LAYERS * D * FF)
    factor = jnp.minimum(1.0, 0.5 * lax.rsqrt(jnp.sum(ss[...]) / count + 1e-30))
    for i in range(3):
        w, m, v = ins[3 * i : 3 * i + 3]
        new_w, new_m, new_v = outs[3 * i : 3 * i + 3]
        grad = jnp.concatenate([g[half, 0, :, i].reshape(D, SUB) for half in range(2)], 1).astype(F32) * factor
        if i == 2:
            grad = grad.T
        mm = 0.9 * m[0] + 0.1 * grad
        vv = 0.95 * v[0] + 0.05 * grad * grad
        wide = w[0].astype(F32)
        new_m[0] = mm
        new_v[0] = vv
        new_w[0] = (wide - 0.02 * (mm * lax.rsqrt(vv + 1e-8) + 0.1 * wide)).astype(BF)


def solution(mesh):
    any_ = pl.BlockSpec(memory_space=pl.ANY)
    chunk_of = (3, HALF, SUB)
    dma = pltpu.SemaphoreType.DMA

    gradients = pl.pallas_call(
        step_kernel,
        name="gradients",
        out_shape=(
            jax.ShapeDtypeStruct((PARTS, RING, 2, *chunk_of), BF),
            jax.ShapeDtypeStruct((8, SUB), F32),
        ),
        in_specs=[any_] * 5,
        out_specs=(any_, pl.BlockSpec(memory_space=pltpu.VMEM)),
        scratch_shapes=[
            pltpu.VMEM((T, D), BF), pltpu.VMEM((T, D), BF), pltpu.VMEM((D, T), BF), pltpu.VMEM((T, D), BF), pltpu.VMEM((D, T), BF),
            pltpu.VMEM((T, D), F32),
            pltpu.VMEM((T, TILE), BF), pltpu.VMEM((T, 2 * TILE), BF),
            pltpu.VMEM((2, D, 2 * TILE), BF), pltpu.VMEM((2, TILE, D), BF),
            pltpu.VMEM((PARTS, RING, 2, *chunk_of), BF),
            pltpu.VMEM((PARTS, RING, *chunk_of), BF),
            pltpu.VMEM((PARTS, RING - 1, *chunk_of), BF),
            pltpu.VMEM((PARTS, RING, 8, SUB), F32),
            dma((2, 6)), dma((2,)), dma((PARTS, RING)),
            dma((PARTS, RING)), dma((PARTS, RING)),
            dma((PARTS, RING - 1)), dma((PARTS, RING - 1)),
            dma((PARTS, RING, 3)), dma((PARTS, RING, 3)),
            dma((PARTS, RING)), dma((PARTS, RING)), pltpu.SemaphoreType.REGULAR((PARTS,)),
        ],
        compiler_params=pltpu.CompilerParams(collective_id=0, has_side_effects=True, vmem_limit_bytes=67_043_328),
    )

    wide = pl.BlockSpec((1, D, TILE), lambda l, p: (l, 0, p))
    tall = pl.BlockSpec((1, TILE, D), lambda l, p: (l, p, 0))
    specs = [wide] * 6 + [tall] * 3
    up_shape, down_shape = (LAYERS, D, FF), (LAYERS, FF, D)
    shapes = [jax.ShapeDtypeStruct(s, t) for s in (up_shape, up_shape, down_shape) for t in (BF, F32, F32)]
    update = pl.pallas_call(
        update_kernel,
        name="update",
        grid=(LAYERS, RING),
        out_shape=shapes,
        in_specs=[pl.BlockSpec((8, SUB), lambda l, p: (0, 0)), pl.BlockSpec((2, 1, 2, *chunk_of), lambda l, p: (1 - l, p, 0, 0, 0, 0))] + specs,
        out_specs=specs,
        compiler_params=pltpu.CompilerParams(vmem_limit_bytes=60_000_000),
    )

    def step(x, dy, wg, wu, wd, mg, mu, md, vg, vu, vd):
        g, ss = gradients(x[0], dy[0], wg, wu, wd)
        new = update(ss, g, wg, mg, vg, wu, mu, vu, wd, md, vd)
        return tuple(new[3 * i + which] for which in range(3) for i in range(3))

    return jax.shard_map(
        step,
        mesh=mesh,
        in_specs=(P(("rep", "dp"), None, None),) * 2 + (P(None, None, None),) * 9,
        out_specs=(P("rep", None, None),) * 9,
        check_vma=False,
    )
```

time: 339 us -> 288 us (0.85)
  Pallas kernels: 338 us -> 287 us
    pallas_call x1, Pallas kernels: 281 us -> 230 us  [step(): g, ss = gradients(x[0], dy[0], wg, wu, wd)]
where the time goes in v2:
time: 288 us
  Pallas kernels  287 us (100%)
    pallas_call x1, Pallas kernels, step(): g, ss = gradients(x[0], dy[0], wg, wu, wd)  230 us
    pallas_call x1, Pallas kernels, step(): new = update(ss, g, wg, mg, vg, wu, mu, vu, wd, md, vd)  57.1 us

profile of v2, /device:TPU:0, one launch (start us, length us, event | category | flops | bytes accessed | tf_op | source)
XLA Modules:
  0.0 287.8 jit_solution(2101227021591601107)
XLA Ops:
  0.6 229.9 %gradients.1 = (bf16[4,8,2,3,320,128]{5,4,3,2,1,0:T(8,128)(2,1)}, f32[8,128]{1,0:T(8,128)}) custom-call(bf16[2048,640]{1,0:T(8,128)(2,1)} %bitcast.2, bf16[2048,640]{1,0:T(8,128)(2,1)} %bitcast.3, bf16[2,640,2048]{2,1,0:T(8,128)(2,1)} %refs_0_.1, bf16[2,640,2048]{2,1,0:T(8,128)(2,1)} %refs_3_.1, bf16[2,2048,640]{2,1,0:T(8,128)(2,1)} %refs_6_.1), custom_call_target="tpu_custom_call" | custom-call | tf_op jit(solution)/shard_map/gradients/pallas_call | solution.py:475
  230.6 57.1 %update.1 = (bf16[2,640,2048]{2,1,0:T(8,128)(2,1)}, f32[2,640,2048]{2,1,0:T(8,128)}, f32[2,640,2048]{2,1,0:T(8,128)}, bf16[2,640,2048]{2,1,0:T(8,128)(2,1)}, f32...) custom-call(f32[8,128]{1,0:T(8,128)} %get-tuple-element.20.ss, ...), custom_call_target="tpu_custom_call" | custom-call | tf_op jit(solution)/shard_map/update/pallas_call | solution.py:476

commit v3 on v2

v3 whole, which is shorter than its diff:
```python
import jax
import jax.numpy as jnp
from jax import lax
from jax.experimental import pallas as pl
from jax.experimental.pallas import tpu as pltpu
from jax.sharding import PartitionSpec as P

T, D, FF, LAYERS = 2048, 640, 2048, 2
RING = 8
TILE = FF // RING
HALF = D // 2
SUB = TILE // 2
PARTS = 2 * LAYERS
ROWS, FEW = 1024, 512
BF, F32 = jnp.bfloat16, jnp.float32
MESH = pl.DeviceIdType.MESH


def rem(a, b):
    return a % b if isinstance(a, int) else lax.rem(a, jnp.int32(b))


def div(a, b):
    return a // b if isinstance(a, int) else lax.div(a, jnp.int32(b))


def dot(a, b, ca, cb):
    return lax.dot_general(a, b, (((ca,), (cb,)), ((), ())), preferred_element_type=F32)


def step_kernel(
    x_hbm, dy_hbm, wg_hbm, wu_hbm, wd_hbm, g_out, ss_out, kept,
    H, A, AT, DY, DYT, ACC, HID, DGU, WGU, WD, G, R, L, PS,
    wsem, xsem, osem, ksem, p_s, p_r, rs_s, rs_r, ag_s, ag_r, ap_s, ap_r, free,
):
    me = lax.axis_index("dp")
    core = rem(me, 2)
    y, z = div(me, 8), rem(div(me, 2), 4)
    pos = z + y * (7 - 2 * z)

    def device(position, c):
        yy = div(position, 4)
        zz = position - yy * (2 * position - 7)
        return {"dp": yy * 8 + zz * 2 + c}

    partner = device(pos, 1 - core)

    def chunk(k):
        return rem(pos + 8 + (4 - div(k + 1, 2)) * (2 * rem(k, 2) - 1), RING)

    def weight_copies(layer, n):
        slot, half = rem(n, 2), div(n, 4)
        copies = []
        for j in range(2):
            at = pl.ds(pl.multiple_of(chunk(rem(2 * n + j, RING)) * TILE + half * SUB, SUB), SUB)
            here = pl.ds(j * SUB, SUB)
            copies += [
                pltpu.make_async_copy(wg_hbm.at[layer, :, at], WGU.at[slot, :, here], wsem.at[slot, 3 * j]),
                pltpu.make_async_copy(wu_hbm.at[layer, :, at], WGU.at[slot, :, pl.ds(TILE + j * SUB, SUB)], wsem.at[slot, 3 * j + 1]),
                pltpu.make_async_copy(wd_hbm.at[layer, at, :], WD.at[slot, here, :], wsem.at[slot, 3 * j + 2]),
            ]
        return copies

    def start_weights(layer, k):
        for c in weight_copies(layer, k):
            c.start()

    def next_weights(layer, k):
        for c in weight_copies(layer, k):
            c.wait()

        @pl.when(k < RING - 1)
        def _():
            start_weights(layer, k + 1)

    x_copy = pltpu.make_async_copy(x_hbm, H, xsem.at[0])
    dy_copy = pltpu.make_async_copy(dy_hbm, DY, xsem.at[1])
    x_copy.start()
    dy_copy.start()
    start_weights(0, 0)

    barrier = pltpu.get_barrier_semaphore()
    for other in (partner, device(rem(pos + 1, RING), core), device(rem(pos + 7, RING), core)):
        pl.semaphore_signal(barrier, inc=1, device_id=other, device_id_type=MESH)

    def rows(r, n=ROWS):
        return pl.ds(pl.multiple_of(r * n, n), n)

    def normed_into(dst):
        @pl.loop(0, T // FEW)
        def _(r):
            at = rows(r, FEW)
            wide = H[at, :].astype(F32)
            scale = lax.rsqrt(jnp.mean(wide * wide, -1, keepdims=True) + 1e-6)
            dst[at, :] = (wide * scale).astype(BF)

    def transposed_into(dst, src):
        @pl.loop(0, T // FEW)
        def _(r):
            at = rows(r, FEW)
            dst[:, at] = src[at, :].T

    def partner_copy(part, k):
        p = chunk(k)
        return pltpu.make_async_remote_copy(
            src_ref=G.at[part, p, 1 - core], dst_ref=R.at[part, p],
            send_sem=p_s.at[part, k], recv_sem=p_r.at[part, k], device_id=partner, device_id_type=MESH,
        )

    def ring_copy(part, k, m, sign):
        return pltpu.make_async_remote_copy(
            src_ref=R.at[part, chunk(k), m], dst_ref=L.at[part, k, m],
            send_sem=rs_s.at[part, k, m], recv_sem=rs_r.at[part, k, m],
            device_id=device(rem(pos + RING + sign, RING), core), device_id_type=MESH,
        )

    def add_up(part, k, m, came):
        p = chunk(k)

        @pl.loop(0, HALF // 64)
        def _(r):
            at = rows(r, 64)
            total = G[part, p, core, m, at, :].astype(F32) + R[part, p, m, at, :].astype(F32)
            for j in came:
                total += L[part, j, m, at, :].astype(F32)
            R[part, p, m, at, :] = total.astype(BF)

    def reduce_step(part, k):
        partner_copy(part, k).wait()

        @pl.loop(0, 3)
        def _(m):
            @pl.when((k == 0) | ((k == 1) & (core == 1)) | ((k == 2) & (core == 0)))
            def _():
                add_up(part, k, m, ())

            @pl.when((k == 1) & (core == 0) | (k == 2) & (core == 1))
            def _():
                ring_copy(part, 0, m, 1).wait_recv()
                add_up(part, k, m, (0,))

            @pl.when(k >= 3)
            def _():
                ring_copy(part, k - 2, m, 1).wait_recv()
                add_up(part, k, m, (k - 2,))

            @pl.when(k == 0)
            def _():
                ring_copy(part, k, m, 1 - 2 * core).start()

            @pl.when(k > 0)
            def _():
                ring_copy(part, k, m, 2 * rem(k, 2) - 1).start()

    def reduce_last(part):
        partner_copy(part, 7).wait()
        pl.semaphore_signal(free.at[part], inc=1, device_id=partner, device_id_type=MESH)

        @pl.loop(0, 3)
        def _(m):
            ring_copy(part, 5, m, 1).wait_recv()
            ring_copy(part, 6, m, 1).wait_recv()

            @pl.loop(0, HALF // 64)
            def _(r):
                at = rows(r, 64)
                total = G[part, pos, core, m, at, :].astype(F32) + R[part, pos, m, at, :].astype(F32)
                total += L[part, 5, m, at, :].astype(F32)
                total += L[part, 6, m, at, :].astype(F32)
                G[part, pos, core, m, at, :] = total.astype(BF)

            gather_copy(part, 1, m, pos, 1).start()
            gather_copy(part, 2, m, pos, -1).start()

        pl.semaphore_wait(free.at[part], 1)
        share_copy(part, 0, core).start()

    def event_chunk(e):
        return rem(pos + 8 + div(e + 1, 2) * (1 - 2 * rem(e, 2)), RING)

    def gather_copy(part, e, m, p, sign):
        return pltpu.make_async_remote_copy(
            src_ref=G.at[part, p, core, m], dst_ref=G.at[part, p, core, m],
            send_sem=ag_s.at[part, e, m], recv_sem=ag_r.at[part, e, m],
            device_id=device(rem(pos + RING + sign, RING), core), device_id_type=MESH,
        )

    def share_copy(part, e, c):
        p = event_chunk(e)
        return pltpu.make_async_remote_copy(
            src_ref=G.at[part, p, c], dst_ref=G.at[part, p, c],
            send_sem=ap_s.at[part, e], recv_sem=ap_r.at[part, e], device_id=partner, device_id_type=MESH,
        )

    def gather_event(part, e):
        p = event_chunk(e)

        @pl.loop(0, 3)
        def _(m):
            gather_copy(part, e, m, p, 1).wait_recv()

            @pl.when((e <= 4) | ((e == 5) & (core == 0)))
            def _():
                gather_copy(part, e + 2, m, p, 2 * rem(e, 2) - 1).start()

            @pl.when((e == 6) & (core == 1))
            def _():
                gather_copy(part, 7, m, p, -1).start()

        share_copy(part, e, core).start()

    def out_copy(part, e):
        p = event_chunk(e)
        return pltpu.make_async_copy(G.at[part, p], g_out.at[part, p], osem.at[part, e])

    def squares(part, e):
        share_copy(part, e, 1 - core).wait_recv()
        out_copy(part, e).start()
        p = event_chunk(e)
        total = jnp.zeros((8, SUB), F32)
        for c in range(2):

            def add(i, total):
                wide = G[part, p, c, div(i, 5), rows(rem(i, 5), 64), :].astype(F32)
                return total + jnp.sum((wide * wide).reshape(8, 8, SUB), 0)

            total = lax.fori_loop(0, 3 * HALF // 64, add, total)
        PS[part, p] = total

    x_copy.wait()
    normed_into(A)

    @pl.loop(0, RING)
    def _(k):
        next_weights(0, k)
        slot = rem(k, 2)

        @pl.loop(0, T // ROWS)
        def _(r):
            at = rows(r)
            both = dot(A[at, :], WGU[slot], 1, 0)
            gate, up = both[:, :TILE], both[:, TILE:]
            hid = (gate * jax.nn.sigmoid(gate) * up).astype(BF)
            part = dot(hid, WD[slot], 1, 0)

            @pl.when(k == 0)
            def _():
                ACC[at, :] = part

            @pl.when(k > 0)
            def _():
                ACC[at, :] += part

    start_weights(1, 0)

    @pl.loop(0, T // FEW)
    def _(r):
        at = rows(r, FEW)
        H[at, :] = (H[at, :].astype(F32) + ACC[at, :].astype(BF).astype(F32)).astype(BF)

    normed_into(A)
    transposed_into(AT, A)
    dy_copy.wait()
    transposed_into(DYT, DY)

    def tile(layer, n, midway, after):
        part = 2 * (1 - layer) + div(n, 4)
        next_weights(layer, n)
        slot = rem(n, 2)
        if layer == 1:

            @pl.when(n > 1)
            def _():
                keep_copy(n - 2).wait()

        @pl.loop(0, T // ROWS)
        def _(r):
            at = rows(r)
            both = dot(A[at, :], WGU[slot], 1, 0)
            gate, up = both[:, :TILE], both[:, TILE:]
            by_hid = dot(DY[at, :], WD[slot], 1, 1).astype(BF).astype(F32)
            sig = jax.nn.sigmoid(gate)
            silu = gate * sig
            HID[at, :] = (silu * up).astype(BF)
            DGU[slot, at, pl.ds(TILE, TILE)] = (by_hid * silu).astype(BF)
            DGU[slot, at, pl.ds(0, TILE)] = (by_hid * up * (sig + silu * (1.0 - sig))).astype(BF)

        if layer == 1:
            keep_copy(n).start()

        at_turn(n, midway)

        for left, right, ms in ((AT, DGU.at[slot], (0, 1)), (DYT, HID, (2,))):
            g = dot(left[...], right[...], 1, 0).astype(BF)
            for i, m in enumerate(ms):
                for j in range(2):
                    at = slice(i * TILE + j * SUB, i * TILE + (j + 1) * SUB)
                    for half in range(2):
                        G[part, chunk(rem(2 * n + j, RING)), half, m] = g[half * HALF : (half + 1) * HALF, at]

        for j in range(2):
            partner_copy(part, rem(2 * n + j, RING)).start()

        at_turn(n, after)

    def keep_copy(n):
        return pltpu.make_async_copy(DGU.at[rem(n, 2)], kept.at[n], ksem.at[rem(n, 2)])

    def fetch_copy(n):
        return pltpu.make_async_copy(kept.at[n], DGU.at[rem(n, 2)], ksem.at[rem(n, 2)])

    def at_turn(n, then):
        for turn, calls in then.items():

            @pl.when(n == turn)
            def _(calls=calls):
                for call, part, *rest in calls:
                    call(part, *rest)

    def one(call, part, odd):
        return call, part, odd + core

    def other(call, part, odd):
        return call, part, odd + 1 - core

    step_, last, gather = reduce_step, reduce_last, gather_event
    pl.semaphore_wait(barrier, 3)

    @pl.loop(0, RING)
    def _(n):
        tile(
            1, n,
            {
                1: [(step_, 0, 0)],
                3: [other(step_, 0, 1)],
                4: [one(step_, 0, 3)],
                5: [(step_, 1, 0)],
                6: [other(step_, 0, 5)],
                7: [other(step_, 1, 1)],
            },
            {
                2: [one(step_, 0, 1)],
                4: [other(step_, 0, 3)],
                5: [one(step_, 0, 5)],
                6: [one(step_, 1, 1)],
                7: [(last, 0)],
            },
        )

    start_weights(1, 0)
    keep_copy(6).wait()
    fetch_copy(0).start()
    keep_copy(7).wait()

    @pl.loop(0, RING)
    def _(n):
        next_weights(1, n)
        fetch_copy(n).wait()

        @pl.when(n < RING - 1)
        def _():
            fetch_copy(n + 1).start()

        slot = rem(n, 2)

        @pl.loop(0, T // ROWS)
        def _(r):
            at = rows(r)
            term = dot(DGU[slot, at, :], WGU[slot], 1, 1)

            @pl.when(n == 0)
            def _():
                ACC[at, :] = term

            @pl.when(n > 0)
            def _():
                ACC[at, :] += term

        at_turn(n, {
            0: [one(step_, 1, 3)],
            1: [other(step_, 1, 3)],
            2: [one(gather, 0, 1)],
            3: [one(step_, 1, 5), other(gather, 0, 1)],
            4: [other(step_, 1, 5)],
            5: [one(gather, 0, 3)],
            6: [other(gather, 0, 3)],
            7: [(last, 1)],
        })

    start_weights(0, 0)

    @pl.loop(0, T // FEW)
    def _(r):
        at = rows(r, FEW)
        by_a = ACC[at, :].astype(BF).astype(F32)
        wide = H[at, :].astype(F32)
        scale = lax.rsqrt(jnp.mean(wide * wide, -1, keepdims=True) + 1e-6)
        along = jnp.mean(by_a * wide, -1, keepdims=True) * (scale * scale)
        by_h = (scale * (by_a - wide * along)).astype(BF).astype(F32)
        DY[at, :] = (DY[at, :].astype(F32) + by_h).astype(BF)

    again = pltpu.make_async_copy(x_hbm, H, xsem.at[0])
    again.start()
    transposed_into(DYT, DY)
    gather_event(0, 5 + core)
    again.wait()
    normed_into(A)
    transposed_into(AT, A)

    @pl.loop(0, RING)
    def _(n):
        tile(
            0, n,
            {
                0: [other(gather, 0, 5), one(gather, 1, 1)],
                1: [(step_, 2, 0), (gather, 0, 7)],
                2: [other(gather, 1, 3)],
                3: [other(step_, 2, 1), one(gather, 1, 5)],
                4: [one(step_, 2, 3)],
                5: [(step_, 3, 0)],
                6: [other(step_, 2, 5)],
                7: [other(step_, 3, 1)],
            },
            {
                0: [other(gather, 1, 1)],
                1: [one(gather, 1, 3)],
                2: [one(step_, 2, 1)],
                3: [other(gather, 1, 5)],
                4: [other(step_, 2, 3), (gather, 1, 7)],
                5: [one(step_, 2, 5)],
                6: [one(step_, 3, 1)],
                7: [(last, 2), one(step_, 3, 3), other(step_, 3, 3)],
            },
        )

    def all_squares(part, first, end):
        @pl.loop(first, end)
        def _(e):
            squares(part, e)

    def both_ways(call, part, odd):
        call(part, odd + core)
        call(part, odd + 1 - core)

    all_squares(0, 0, 8)
    both_ways(reduce_step, 3, 5)
    both_ways(gather_event, 2, 1)
    all_squares(1, 0, 8)
    reduce_last(3)
    both_ways(gather_event, 2, 3)
    all_squares(2, 0, 3)
    both_ways(gather_event, 3, 1)
    both_ways(gather_event, 2, 5)
    both_ways(gather_event, 3, 3)
    gather_event(2, 7)
    all_squares(2, 3, 7)
    all_squares(3, 0, 3)
    both_ways(gather_event, 3, 5)
    squares(2, 7)
    all_squares(3, 3, 5)
    gather_event(3, 7)
    all_squares(3, 5, 8)

    total = jnp.zeros((8, SUB), F32)
    for part in range(PARTS):
        for p in range(RING):
            total += PS[part, p]
    ss_out[...] = total

    for part in range(PARTS):

        @pl.loop(0, RING)
        def _(k):
            share_copy(part, k, core).wait_send()
            out_copy(part, k).wait()

        @pl.loop(0, RING - 1)
        def _(k):
            for m in range(3):
                ring_copy(part, k, m, 1).wait_send()
                gather_copy(part, k + 1, m, event_chunk(k + 1), 1).wait_send()


def update_kernel(ss, g, *refs):
    ins, outs = refs[:9], refs[9:]
    count = float(3 * LAYERS * D * FF)
    factor = jnp.minimum(1.0, 0.5 * lax.rsqrt(jnp.sum(ss[...]) / count + 1e-30))
    for i in range(3):
        w, m, v = ins[3 * i : 3 * i + 3]
        new_w, new_m, new_v = outs[3 * i : 3 * i + 3]
        grad = jnp.concatenate([g[half, 0, :, i].reshape(D, SUB) for half in range(2)], 1).astype(F32) * factor
        if i == 2:
            grad = grad.T
        mm = 0.9 * m[0] + 0.1 * grad
        vv = 0.95 * v[0] + 0.05 * grad * grad
        wide = w[0].astype(F32)
        new_m[0] = mm
        new_v[0] = vv
        new_w[0] = (wide - 0.02 * (mm * lax.rsqrt(vv + 1e-8) + 0.1 * wide)).astype(BF)


def solution(mesh):
    any_ = pl.BlockSpec(memory_space=pl.ANY)
    chunk_of = (3, HALF, SUB)
    dma = pltpu.SemaphoreType.DMA

    gradients = pl.pallas_call(
        step_kernel,
        name="gradients",
        out_shape=(
            jax.ShapeDtypeStruct((PARTS, RING, 2, *chunk_of), BF),
            jax.ShapeDtypeStruct((8, SUB), F32),
            jax.ShapeDtypeStruct((RING, T, 2 * TILE), BF),
        ),
        in_specs=[any_] * 5,
        out_specs=(any_, pl.BlockSpec(memory_space=pltpu.VMEM), any_),
        scratch_shapes=[
            pltpu.VMEM((T, D), BF), pltpu.VMEM((T, D), BF), pltpu.VMEM((D, T), BF), pltpu.VMEM((T, D), BF), pltpu.VMEM((D, T), BF),
            pltpu.VMEM((T, D), F32),
            pltpu.VMEM((T, TILE), BF), pltpu.VMEM((2, T, 2 * TILE), BF),
            pltpu.VMEM((2, D, 2 * TILE), BF), pltpu.VMEM((2, TILE, D), BF),
            pltpu.VMEM((PARTS, RING, 2, *chunk_of), BF),
            pltpu.VMEM((PARTS, RING, *chunk_of), BF),
            pltpu.VMEM((PARTS, RING - 1, *chunk_of), BF),
            pltpu.VMEM((PARTS, RING, 8, SUB), F32),
            dma((2, 6)), dma((2,)), dma((PARTS, RING)), dma((2,)),
            dma((PARTS, RING)), dma((PARTS, RING)),
            dma((PARTS, RING - 1, 3)), dma((PARTS, RING - 1, 3)),
            dma((PARTS, RING, 3)), dma((PARTS, RING, 3)),
            dma((PARTS, RING)), dma((PARTS, RING)), pltpu.SemaphoreType.REGULAR((PARTS,)),
        ],
        compiler_params=pltpu.CompilerParams(collective_id=0, has_side_effects=True, vmem_limit_bytes=67_043_328),
    )

    wide = pl.BlockSpec((1, D, TILE), lambda l, p: (l, 0, p))
    tall = pl.BlockSpec((1, TILE, D), lambda l, p: (l, p, 0))
    specs = [wide] * 6 + [tall] * 3
    up_shape, down_shape = (LAYERS, D, FF), (LAYERS, FF, D)
    shapes = [jax.ShapeDtypeStruct(s, t) for s in (up_shape, up_shape, down_shape) for t in (BF, F32, F32)]
    update = pl.pallas_call(
        update_kernel,
        name="update",
        grid=(LAYERS, RING),
        out_shape=shapes,
        in_specs=[pl.BlockSpec((8, SUB), lambda l, p: (0, 0)), pl.BlockSpec((2, 1, 2, *chunk_of), lambda l, p: (1 - l, p, 0, 0, 0, 0))] + specs,
        out_specs=specs,
        compiler_params=pltpu.CompilerParams(vmem_limit_bytes=60_000_000),
    )

    def step(x, dy, wg, wu, wd, mg, mu, md, vg, vu, vd):
        g, ss, _ = gradients(x[0], dy[0], wg, wu, wd)
        new = update(ss, g, wg, mg, vg, wu, mu, vu, wd, md, vd)
        return tuple(new[3 * i + which] for which in range(3) for i in range(3))

    return jax.shard_map(
        step,
        mesh=mesh,
        in_specs=(P(("rep", "dp"), None, None),) * 2 + (P(None, None, None),) * 9,
        out_specs=(P("rep", None, None),) * 9,
        check_vma=False,
    )
```

time: 288 us -> 281 us (0.976)
  Pallas kernels: 287 us -> 280 us
    pallas_call x1, Pallas kernels: 230 us -> 223 us  [step(): g, ss, _ = gradients(x[0], dy[0], wg, wu, wd)]
where the time goes in v3:
time: 281 us
  Pallas kernels  280 us (100%)
    pallas_call x1, Pallas kernels, step(): g, ss, _ = gradients(x[0], dy[0], wg, wu, wd)  223 us
    pallas_call x1, Pallas kernels, step(): new = update(ss, g, wg, mg, vg, wu, mu, vu, wd, md, vd)  57 us

profile of v3, /device:TPU:0, one launch (start us, length us, event | category | flops | bytes accessed | tf_op | source)
XLA Modules:
  0.0 280.7 jit_solution(3568600135509376073)
XLA Ops:
  0.6 222.8 %gradients.1 = (bf16[4,8,2,3,320,128]{5,4,3,2,1,0:T(8,128)(2,1)}, f32[8,128]{1,0:T(8,128)}, bf16[8,2048,512]{2,1,0:T(8,128)(2,1)}) custom-call(bf16[2048,640]{1,0:T(8,128)(2,1)} %bitcast.2, bf16[2048,640]{1,0:T(8,128)(2,1)} %bitcast.3, bf16[2,640,2048]{2,1,0:T(8,128)(2,1)} %refs_0_.1, bf16[2,640,2048]{2,1,0:T(8,128)(2,1)} %refs_3_.1, ...), custom_call_target="tpu_custom_call" | custom-call | tf_op jit(solution)/shard_map/gradients/pallas_call | solution.py:551
  223.5 57.0 %update.1 = (bf16[2,640,2048]{2,1,0:T(8,128)(2,1)}, f32[2,640,2048]{2,1,0:T(8,128)}, f32[2,640,2048]{2,1,0:T(8,128)}, bf16[2,640,2048]{2,1,0:T(8,128)(2,1)}, f32...) custom-call(f32[8,128]{1,0:T(8,128)} %get-tuple-element.20.ss, ...), custom_call_target="tpu_custom_call" | custom-call | tf_op jit(solution)/shard_map/update/pallas_call | solution.py:552

commit v4 on v3

--- a/solution.py
+++ b/solution.py
@@ -220,11 +220,11 @@
         total = jnp.zeros((8, SUB), F32)
         for c in range(2):
 
-            def add(i, total):
-                wide = G[part, p, c, div(i, 5), rows(rem(i, 5), 64), :].astype(F32)
-                return total + jnp.sum((wide * wide).reshape(8, 8, SUB), 0)
-
-            total = lax.fori_loop(0, 3 * HALF // 64, add, total)
+            def add(m, total):
+                wide = G[part, p, c, m].astype(F32)
+                return total + jnp.sum((wide * wide).reshape(HALF // 8, 8, SUB), 0)
+
+            total = lax.fori_loop(0, 3, add, total)
         PS[part, p] = total
 
     x_copy.wait()
@@ -235,9 +235,9 @@
         next_weights(0, k)
         slot = rem(k, 2)
 
-        @pl.loop(0, T // ROWS)
+        @pl.loop(0, T // 2048)
         def _(r):
-            at = rows(r)
+            at = rows(r, 2048)
             both = dot(A[at, :], WGU[slot], 1, 0)
             gate, up = both[:, :TILE], both[:, TILE:]
             hid = (gate * jax.nn.sigmoid(gate) * up).astype(BF)
@@ -414,22 +414,22 @@
             {
                 0: [other(gather, 0, 5), one(gather, 1, 1)],
                 1: [(step_, 2, 0), (gather, 0, 7)],
-                2: [other(gather, 1, 3)],
-                3: [other(step_, 2, 1), one(gather, 1, 5)],
-                4: [one(step_, 2, 3)],
-                5: [(step_, 3, 0)],
-                6: [other(step_, 2, 5)],
-                7: [other(step_, 3, 1)],
+                2: [one(step_, 2, 1), other(gather, 1, 3)],
+                3: [one(step_, 2, 3), one(gather, 1, 5)],
+                4: [one(step_, 2, 5)],
+                5: [(step_, 3, 0), (gather, 1, 7)],
+                6: [one(step_, 3, 1)],
+                7: [one(step_, 3, 3), one(gather, 2, 1)],
             },
             {
                 0: [other(gather, 1, 1)],
                 1: [one(gather, 1, 3)],
-                2: [one(step_, 2, 1)],
-                3: [other(gather, 1, 5)],
-                4: [other(step_, 2, 3), (gather, 1, 7)],
-                5: [one(step_, 2, 5)],
-                6: [one(step_, 3, 1)],
-                7: [(last, 2), one(step_, 3, 3), other(step_, 3, 3)],
+                2: [other(step_, 2, 1)],
+                3: [other(step_, 2, 3), other(gather, 1, 5)],
+                4: [other(step_, 2, 5)],
+                5: [(last, 2)],
+                6: [other(step_, 3, 1)],
+                7: [other(step_, 3, 3), other(gather, 2, 1)],
             },
         )
 
@@ -444,16 +444,17 @@
 
     all_squares(0, 0, 8)
     both_ways(reduce_step, 3, 5)
-    both_ways(gather_event, 2, 1)
-    all_squares(1, 0, 8)
+    all_squares(1, 0, 6)
+    both_ways(gather_event, 2, 3)
     reduce_last(3)
-    both_ways(gather_event, 2, 3)
+    all_squares(1, 6, 8)
+    both_ways(gather_event, 2, 5)
     all_squares(2, 0, 3)
     both_ways(gather_event, 3, 1)
-    both_ways(gather_event, 2, 5)
+    gather_event(2, 7)
+    all_squares(2, 3, 5)
     both_ways(gather_event, 3, 3)
-    gather_event(2, 7)
-    all_squares(2, 3, 7)
+    all_squares(2, 5, 7)
     all_squares(3, 0, 3)
     both_ways(gather_event, 3, 5)
     squares(2, 7)

time: 281 us -> 273 us (0.972)
  Pallas kernels: 280 us -> 272 us
    pallas_call x1, Pallas kernels: 223 us -> 215 us  [step(): g, ss, _ = gradients(x[0], dy[0], wg, wu, wd)]
where the time goes in v4:
time: 273 us
  Pallas kernels  272 us (100%)
    pallas_call x1, Pallas kernels, step(): g, ss, _ = gradients(x[0], dy[0], wg, wu, wd)  215 us
    pallas_call x1, Pallas kernels, step(): new = update(ss, g, wg, mg, vg, wu, mu, vu, wd, md, vd)  57 us

profile of v4, /device:TPU:0, one launch (start us, length us, event | category | flops | bytes accessed | tf_op | source)
XLA Modules:
  0.0 272.6 jit_solution(11594090871335830570)
XLA Ops:
  0.6 214.7 %gradients.1 = (bf16[4,8,2,3,320,128]{5,4,3,2,1,0:T(8,128)(2,1)}, f32[8,128]{1,0:T(8,128)}, bf16[8,2048,512]{2,1,0:T(8,128)(2,1)}) custom-call(bf16[2048,640]{1,0:T(8,128)(2,1)} %bitcast.2, bf16[2048,640]{1,0:T(8,128)(2,1)} %bitcast.3, bf16[2,640,2048]{2,1,0:T(8,128)(2,1)} %refs_0_.1, bf16[2,640,2048]{2,1,0:T(8,128)(2,1)} %refs_3_.1, ...), custom_call_target="tpu_custom_call" | custom-call | tf_op jit(solution)/shard_map/gradients/pallas_call | solution.py:552
  215.4 57.0 %update.1 = (bf16[2,640,2048]{2,1,0:T(8,128)(2,1)}, f32[2,640,2048]{2,1,0:T(8,128)}, f32[2,640,2048]{2,1,0:T(8,128)}, bf16[2,640,2048]{2,1,0:T(8,128)(2,1)}, f32...) custom-call(f32[8,128]{1,0:T(8,128)} %get-tuple-element.20.ss, ...), custom_call_target="tpu_custom_call" | custom-call | tf_op jit(solution)/shard_map/update/pallas_call | solution.py:553
